TPU v7x, 32 devices: a whole 2x2x4 slice. The times are simulated.
32 devices in a mesh: dp: 4 (over y, x), seq: 2 (over core), head: 4 (over z).
Axes of the slice: x: 2, y: 2, z: 4, core: 2. Of those that a mesh axis runs over, the one named last changes fastest.
Arguments:
- q_lat: bfloat16 [3072, 8192], P(('dp', 'seq'), 'head'), may hold values from -160 to 160
- q_rope: bfloat16 [3072, 1024], P(('dp', 'seq'), 'head'), may hold values from -6 to 6
- grad_out: bfloat16 [3072, 8192], P(('dp', 'seq'), 'head'), may hold values from -6 to 6
- prefix_keys: bfloat16 [576, 512], P(None, 'seq'), may hold values from -6 to 6
- comp_lengths: int32 [3], replicated, may hold values from 128 to 1024, as said below
- prefix_len: int32 [1], replicated, may hold values from 65 to 512
Outputs:
- dq_lat: bfloat16 [3072, 8192], P(('dp', 'seq'), 'head')
- dq_rope: bfloat16 [3072, 1024], P(('dp', 'seq'), 'head')
- d_keys: float32 [576, 512], P(None, ('seq', 'head'))
Inputs may be any that keep to these rules, and one draw needn't show every extreme that they name: `comp_lengths`: each a multiple of 128.
All inputs are finite; a program needn't handle non-finite values.
Results may differ from a plain program's by a relative error of at most 0.0089.
Values may be sent and summed in bfloat16 or wider, within the bound.
A program may use at most 64 MiB of HBM per device.

v0:
```python
import jax
import jax.numpy as jnp
from jax import lax
from jax.sharding import PartitionSpec as P

DL = 512
DR = 64
CLEN = 1024


neg_value = -1e30


def on_device(q_lat, q_rope, grad_out, prefix_keys, comp_lengths, prefix_len):
    tok_rows = q_lat.shape[0]
    heads_here = q_lat.shape[1] // DL
    rows = tok_rows * heads_here
    scale = (DL + DR) ** (-0.5)
    tok_ids = lax.axis_index(("dp", "seq")) * tok_rows + jnp.arange(tok_rows, dtype=jnp.int32)
    comp_ids = tok_ids // CLEN
    table = jnp.arange(comp_lengths.shape[0], dtype=jnp.int32)
    length = jnp.sum(
        jnp.where(comp_ids[:, None] == table[None, :], comp_lengths[None, :], 0), axis=1
    )
    valid = tok_ids % CLEN < length
    query_lat = q_lat.reshape(rows, DL)
    query_rope = q_rope.reshape(rows, DR)
    upstream = jnp.where(
        jnp.repeat(valid, heads_here)[:, None],
        grad_out.reshape(rows, DL),
        jnp.zeros((), jnp.bfloat16),
    )
    limit = prefix_len[0]
    total_keys = prefix_keys.shape[1] * lax.axis_size("seq")
    contract_last = (((1,), (1,)), ((), ()))
    contract_first = (((0,), (0,)), ((), ()))

    def scores_of(piece):
        key_lat = piece[:DL]
        key_rope = piece[DL:]
        scores = (
            jnp.dot(query_lat, key_lat, preferred_element_type=jnp.float32)
            + jnp.dot(query_rope, key_rope, preferred_element_type=jnp.float32)
        ) * scale
        keep = jnp.arange(piece.shape[1], dtype=jnp.int32) < limit
        dprob = jnp.dot(upstream, key_lat, preferred_element_type=jnp.float32)
        return (key_lat, key_rope, scores, keep[None, :], dprob)

    def make_backward(peak, total, delta):

        def backward_step(carry, piece, start):
            key_lat, key_rope, scores, keep, dprob = scores_of(piece)
            prob = jnp.where(
                keep,
                jnp.exp(jnp.where(keep, scores, neg_value) - peak[:, None]) / total[:, None],
                0.0,
            )
            dscore = prob * (dprob - delta[:, None])
            prob_b = prob.astype(jnp.bfloat16)
            dscore_b = dscore.astype(jnp.bfloat16)
            grad_lat = lax.dot_general(
                dscore_b, key_lat, contract_last, preferred_element_type=jnp.float32
            )
            grad_rope = lax.dot_general(
                dscore_b, key_rope, contract_last, preferred_element_type=jnp.float32
            )
            term_lat = lax.dot_general(
                upstream, prob_b, contract_first, preferred_element_type=jnp.float32
            ) + scale * lax.dot_general(
                query_lat, dscore_b, contract_first, preferred_element_type=jnp.float32
            )
            term_rope = scale * lax.dot_general(
                query_rope, dscore_b, contract_first, preferred_element_type=jnp.float32
            )
            update = jnp.concatenate([term_lat, term_rope], axis=0)
            return (grad_lat, grad_rope, update)

        return backward_step

    grads_init = (
        jnp.zeros((rows, DL), jnp.float32),
        jnp.zeros((rows, DR), jnp.float32),
        jnp.zeros((DL + DR, total_keys), jnp.float32),
    )
    peak = jnp.full((rows,), neg_value, jnp.float32)
    total = jnp.zeros((rows,), jnp.float32)
    key_lat, key_rope, scores, keep, dprob = scores_of(
        lax.all_gather(prefix_keys, "seq", axis=1, tiled=True)
    )
    masked = jnp.where(keep, scores, neg_value)
    new_peak = jnp.maximum(peak, jnp.max(masked, axis=1))
    expo = jnp.where(keep, jnp.exp(masked - new_peak[:, None]), 0.0)
    peak = new_peak
    total = jnp.sum(expo, axis=1)
    weighted = jnp.sum(expo * dprob, axis=1)
    backward_step = make_backward(peak, total, weighted / total)
    grad_lat, grad_rope, key_grads = backward_step(
        grads_init, lax.all_gather(prefix_keys, "seq", axis=1, tiled=True), jnp.int32(0)
    )
    by_seq = lax.psum_scatter(key_grads, "seq", scatter_dimension=1, tiled=True)
    portion = lax.psum_scatter(by_seq, "head", scatter_dimension=1, tiled=True)
    d_keys = lax.psum(portion, "dp")
    dq_lat = (scale * grad_lat).astype(jnp.bfloat16).reshape(tok_rows, heads_here * DL)
    dq_rope = (scale * grad_rope).astype(jnp.bfloat16).reshape(tok_rows, heads_here * DR)
    return (dq_lat, dq_rope, d_keys)


def solution(mesh):
    in_specs = (
        P(("dp", "seq"), "head"),
        P(("dp", "seq"), "head"),
        P(("dp", "seq"), "head"),
        P(None, "seq"),
        P(),
        P(),
    )
    out_specs = (P(("dp", "seq"), "head"), P(("dp", "seq"), "head"), P(None, ("seq", "head")))
    return jax.shard_map(
        on_device, mesh=mesh, in_specs=in_specs, out_specs=out_specs, check_vma=False
    )
```

profile of v0, /device:TPU:0, one launch (start us, length us, event | category | flops | bytes accessed | tf_op | source)
XLA Modules:
  0.0 119.2 jit_solution(12004956962151974699)
XLA Ops:
  7.2 0.0 reduce-scatter.5.cloned.1.call-start
  7.9 0.7 select_reduce_fusion.1
  8.7 0.1 broadcast_in_dim.73
  8.8 0.2 broadcast_in_dim.74
  8.9 1.2 reshape.56
  10.1 2.6 %all_gather.4 = bf16[576,512]{1,0:T(8,128)(2,1)S(1)} all-gather(bf16[576,256]{1,0:T(8,128)(2,1)} %param.9), channel_id=1, replica_groups=mesh['dp'=4,'seq'=2,'head'=4] {'seq'}, dimensions={1}, use_global_device_ids=true | all-gather | bytes 884736 | tf_op jit(solution)/shard_map/all_gather | solution.py:98
  12.7 0.0 copy-start
  12.7 2.9 %reshape.55 = bf16[1536,512]{1,0:T(8,128)(2,1)S(1)} reshape(bf16[384,2048]{1,0:T(8,128)(2,1)} %param.6) | data formatting | bytes 3145728 | tf_op jit(solution)/shard_map/reshape | solution.py:26
  15.6 3.7 %reshape.57 = bf16[1536,512]{1,0:T(8,128)(2,1)} reshape(bf16[384,2048]{1,0:T(8,128)(2,1)} %param.8) | data formatting | bytes 3145728 | tf_op jit(solution)/shard_map/reshape | solution.py:30
  19.4 1.0 fusion.12
  20.4 0.0 copy-start.2
  20.4 0.7 fusion.22
  21.2 0.0 copy-done
  21.2 0.6 copy-done.2
  21.8 1.6 %select_reduce_fusion = (f32[1536]{0:T(1024)S(1)}, f32[1536]{0:T(1024)S(1)}, f32[1536,512]{0,1:T(8,128)S(1)}) fusion(f32[1536,512]{0,1:T(8,128)S(1)} %get-tuple-element.18, f32[1536]{0:T(1024)S(1)} %broadcast_maximum_fusion, pred[512]{0:T(512)(128)(4,1)S(1)} %iota_compare_fusion.1, bf16[576,512]{1,0:T(8,128)(2,1)S(1)} %all_gather.4, ...), kind=kOutput, calls=%fused_computation.9 | convolution fusion | flops 810021888 | bytes 8411648 | tf_op jit(solution)/shard_map/dot_general | solution.py:46
  23.4 1.5 %fusion.4 = f32[512,512]{1,0:T(8,128)S(1)} fusion(bf16[1536,512]{1,0:T(8,128)(2,1)S(1)} %copy-done.2, pred[1536]{0:T(1024)(128)(4,1)S(1)} %broadcast_in_dim.74, f32[1536,512]{0,1:T(8,128)S(1)} %get-tuple-element.18, f32[1536]{0:T(1024)S(1)} %get-tuple-element.15, f32[1536]{0:T(1024)S(1)} %broadcast_maximum_fusion, pred[512]{0:T(512)(128)(4,1)S(1)} %iota_compare_fusion.1), kind=kOutput, calls=%fused_computation.12 | convolution fusion | flops 809238528 | bytes 5781504 | tf_op jit(solution)/shard_map/dot_general | solution.py:67
  24.9 0.9 multiply_convert_fusion
  25.8 0.6 fusion.8
  26.4 1.0 fusion.7
  27.4 1.1 pad_maximum_fusion
  28.5 0.0 copy-start.1
  28.5 0.0 reduce-scatter.5.cloned.1.call-update
  28.5 0.0 reduce-scatter.7.cloned.1.call-start
  28.6 11.2 %reduce-scatter.5.cloned.1.call-done = f32[576,256]{1,0:T(8,128)} async-done(((f32[576,512]{1,0:T(8,128)}), f32[576,256]{1,0:T(8,128)}) %reduce-scatter.5.cloned.1.call-update) | async-done | bytes 589840 | tf_op jit(solution)/shard_map/reduce_scatter | solution.py:100
  39.8 2.1 %copy.24 = f32[576,256]{0,1:T(8,128)} copy(f32[576,256]{1,0:T(8,128)} %reduce-scatter.5.cloned.1.call-done) | data formatting | bytes 1179648
  41.9 0.0 reduce-scatter.7.cloned.1.call-update
  41.9 0.0 all-reduce.2.cloned.1.call-start
  42.0 0.0 copy-done.1
  42.0 2.1 %fusion.2 = bf16[1536,512]{0,1:T(8,128)(2,1)} fusion(bf16[1536,512]{0,1:T(8,128)(2,1)S(1)} %multiply_convert_fusion, bf16[576,512]{1,0:T(8,128)(2,1)S(1)} %copy-done.1), kind=kOutput, calls=%fused_computation.8 | convolution fusion | flops 806879232 | bytes 3670016 | tf_op jit(solution)/shard_map/dot_general | solution.py:61
  44.1 1.7 %copy.20 = bf16[1536,512]{1,0:T(8,128)(2,1)S(1)} copy(bf16[1536,512]{0,1:T(8,128)(2,1)} %fusion.2) | data formatting | bytes 3145728 | tf_op jit(solution)/shard_map/convert_element_type | solution.py:103
  45.8 2.2 %reshape.58 = bf16[384,2048]{1,0:T(8,128)(2,1)} reshape(bf16[1536,512]{1,0:T(8,128)(2,1)S(1)} %copy.20) | data formatting | bytes 3145728 | tf_op jit(solution)/shard_map/reshape | solution.py:103
  48.1 17.8 %reduce-scatter.7.cloned.1.call-done = f32[64,576]{1,0:T(8,128)} async-done(((f32[256,576]{1,0:T(8,128)}), f32[64,576]{1,0:T(8,128)}) %reduce-scatter.7.cloned.1.call-update) | async-done | bytes 147472
  65.9 1.8 %copy.25 = f32[576,64]{1,0:T(8,128)} copy(f32[576,64]{0,1:T(8,128)} %bitcast.19) | data formatting | bytes 294912
  67.7 0.0 all-reduce.2.cloned.1.call-update
  67.7 1.2 %fusion.3 = bf16[1536,64]{0,1:T(8,128)(2,1)S(1)} fusion(bf16[1536,512]{0,1:T(8,128)(2,1)S(1)} %multiply_convert_fusion, bf16[576,512]{1,0:T(8,128)(2,1)} %copy-done), kind=kOutput, calls=%fused_computation.11 | convolution fusion | flops 100859904 | bytes 1835008 | tf_op jit(solution)/shard_map/dot_general | solution.py:64
  68.9 0.2 copy.21
  69.2 1.0 reshape.59
  70.1 40.8 %all-reduce.2.cloned.1.call-done = f32[576,64]{1,0:T(8,128)} async-done(((f32[576,64]{1,0:T(8,128)}), f32[576,64]{1,0:T(8,128)}) %all-reduce.2.cloned.1.call-update) | async-done | bytes 147472 | tf_op jit(solution)/shard_map/psum | solution.py:102
  110.9 1.8 %copy.22 = f32[576,64]{0,1:T(8,128)} copy(f32[576,64]{1,0:T(8,128)} %all-reduce.2.cloned.1.call-done) | data formatting | bytes 294912
  (5 shorter events, 0.0 us)
Async XLA Ops:
  7.2 32.6 %reduce-scatter.5.cloned.1.call-start = ((), (), s32[]{:S(2)}) async-start(), calls=%async_computation.2 | async-start | bytes 1769472 | tf_op jit(solution)/shard_map/reduce_scatter | solution.py:100
  12.7 8.5 %copy-start = (bf16[576,512]{1,0:T(8,128)(2,1)}, bf16[576,512]{1,0:T(8,128)(2,1)S(1)}, u32[]{:S(2)}) copy-start(bf16[576,512]{1,0:T(8,128)(2,1)S(1)} %all_gather.4) | copy-start | bytes 1769476
  20.4 1.4 %copy-start.2 = (bf16[1536,512]{1,0:T(8,128)(2,1)S(1)}, bf16[1536,512]{1,0:T(8,128)(2,1)}, u32[]{:S(2)}) copy-start(bf16[1536,512]{1,0:T(8,128)(2,1)} %reshape.57) | copy-start | bytes 4718596
  28.5 13.5 %copy-start.1 = (bf16[576,512]{1,0:T(8,128)(2,1)S(1)}, bf16[576,512]{1,0:T(8,128)(2,1)}, u32[]{:S(2)}) copy-start(bf16[576,512]{1,0:T(8,128)(2,1)} %copy-done) | copy-start | bytes 1769476
  28.5 37.4 %reduce-scatter.7.cloned.1.call-start = ((), (), s32[]{:S(2)}) async-start(), calls=%async_computation.4 | async-start | bytes 819200
  41.9 69.0 %all-reduce.2.cloned.1.call-start = ((), (), s32[]{:S(2)}) async-start(), calls=%async_computation.3 | async-start | bytes 589824 | tf_op jit(solution)/shard_map/psum | solution.py:102
Sparse Core Ops, SparseCore 0:
  28.6 11.0 reduce-scatter.4
  42.1 23.8 reduce-scatter.6
  68.9 41.9 all-reduce.1
where the time goes:
time: 120 us; the launch traced here: 119 us
  waiting for transfers between devices  69.9 us (58%)
  local copies, waits for them, and re-layouts  19.6 us (16%)
  between operations  14.5 us (12%)
  matrix products  9.83 us (8%)
  other arithmetic  2.74 us (2%)
  blocking collectives  2.56 us (2%)
    psum x1, waiting for transfers between devices, on_device(): d_keys = lax.psum(portion, 'dp')  40.8 us
    unnamed x4, waiting for transfers between devices  17.9 us
    reduce_scatter x1, waiting for transfers between devices, on_device(): by_seq = lax.psum_scatter(key_grads, 'seq', scatter_dimension=1, tiled=True)  11.2 us
    unnamed x9, local copies, waits for them, and re-layouts  6.33 us
    reshape x1, local copies, waits for them, and re-layouts, on_device(): grad_out.reshape(rows, DL)  3.73 us
    reshape x1, local copies, waits for them, and re-layouts, on_device(): query_lat = q_lat.reshape(rows, DL)  2.94 us
    all_gather x1, blocking collectives, on_device(): lax.all_gather(prefix_keys, 'seq', axis=1, tiled=True)  2.56 us
  transfers between devices with their start and end apart: 3, of which 3 were waited for; matrix products, arithmetic and copies ran while one was open for 7% of the time, Pallas kernels for 0%

commit v1 on v0

v1 whole, which is shorter than its diff:
```python
import functools

import jax
import jax.numpy as jnp
from jax import lax
from jax.experimental import pallas as pl
from jax.experimental.pallas import tpu as pltpu
from jax.sharding import PartitionSpec as P

DL = 512
DR = 64
CLEN = 1024
MESH = pl.DeviceIdType.MESH
NEG = -1e30
F32 = jnp.float32
BF16 = jnp.bfloat16


def dot(a, b, da, db):
    return lax.dot_general(a, b, (((da,), (db,)), ((), ())), preferred_element_type=F32)


def compute_kernel(tok_rows, lens_ref, plen_ref, q_ref, qr_ref, g_ref, keys_ref,
                   dq_ref, dqr_ref, terms_ref, keys_t, rope_t, acc_p, acc_q, acc_r):
    head = pl.program_id(0)
    parity = lax.rem(head, 2)
    scale = (DL + DR) ** (-0.5)
    cols = keys_ref.shape[1]

    @pl.when(head == 0)
    def _():
        keys_t[...] = keys_ref[:DL].T
        rope = keys_ref[DL:].astype(F32).T
        zero = jnp.zeros_like(rope)
        rope_t[0] = jnp.concatenate([rope, zero], axis=1).astype(BF16)
        rope_t[1] = jnp.concatenate([zero, rope], axis=1).astype(BF16)
        acc_p[...] = jnp.zeros_like(acc_p)
        acc_q[...] = jnp.zeros_like(acc_q)
        acc_r[...] = jnp.zeros_like(acc_r)

    first = (lax.axis_index("dp") * lax.axis_size("seq") + lax.axis_index("seq")) * tok_rows
    tok = first + lax.broadcasted_iota(jnp.int32, (tok_rows, 1), 0)
    comp = tok // CLEN
    length = jnp.zeros_like(tok)
    for c in range(lens_ref.shape[0]):
        length = jnp.where(comp == c, lens_ref[c], length)
    valid = tok - comp * CLEN < length
    g = jnp.where(valid, g_ref[...].astype(F32), 0.0).astype(BF16)
    q = q_ref[...]
    qr = qr_ref[...]
    kt = keys_t[...]
    rt = rope_t[parity]
    s = (dot(kt, q, 1, 1) + dot(rt, qr, 1, 1)) * scale
    keep = lax.broadcasted_iota(jnp.int32, (cols, 1), 0) < plen_ref[0]
    s = jnp.where(keep, s, NEG)
    e = jnp.exp(s - jnp.max(s, axis=0, keepdims=True))
    inv = 1.0 / jnp.sum(e, axis=0, keepdims=True)
    dp = dot(kt, g, 1, 1)
    p = e * inv
    delta = jnp.sum(p * dp, axis=0, keepdims=True)
    ds = (p * (dp - delta)).astype(BF16)
    acc_p[...] += dot(p.astype(BF16), g, 1, 0)
    acc_q[...] += dot(ds, q, 1, 0)
    acc_r[parity] += dot(ds, qr, 1, 0)
    dst = ds.T
    dq_ref[...] = (scale * dot(dst, kt, 1, 0)).astype(BF16)
    half = (scale * dot(dst, rt, 1, 0)).astype(BF16)

    @pl.when(parity == 0)
    def _():
        dqr_ref[...] = half

    @pl.when(parity == 1)
    def _():
        dqr_ref[...] += half

    @pl.when(head == pl.num_programs(0) - 1)
    def _():
        terms_ref[:, :DL] = (acc_p[...] + scale * acc_q[...]).astype(BF16)
        terms_ref[:, DL:] = (scale * (acc_r[0][:, :DR] + acc_r[1][:, DR:])).astype(BF16)


def compute(q_lat, q_rope, grad_out, keys, comp_lengths, prefix_len):
    tok_rows = q_lat.shape[0]
    heads = q_lat.shape[1] // DL
    cols = keys.shape[1]
    lat = pl.BlockSpec((tok_rows, DL), lambda h: (0, h))
    rope = pl.BlockSpec((tok_rows, 2 * DR), lambda h: (0, h // 2))
    smem = pl.BlockSpec(memory_space=pltpu.SMEM)
    return pl.pallas_call(
        functools.partial(compute_kernel, tok_rows),
        grid=(heads,),
        out_shape=(
            jax.ShapeDtypeStruct(q_lat.shape, BF16),
            jax.ShapeDtypeStruct(q_rope.shape, BF16),
            jax.ShapeDtypeStruct((cols, DL + DR), BF16),
        ),
        in_specs=[smem, smem, lat, rope, lat, pl.BlockSpec((DL + DR, cols), lambda h: (0, 0))],
        out_specs=(lat, rope, pl.BlockSpec((cols, DL + DR), lambda h: (0, 0))),
        scratch_shapes=[
            pltpu.VMEM((cols, DL), BF16),
            pltpu.VMEM((2, cols, 2 * DR), BF16),
            pltpu.VMEM((cols, DL), F32),
            pltpu.VMEM((cols, DL), F32),
            pltpu.VMEM((2, cols, 2 * DR), F32),
        ],
        compiler_params=pltpu.CompilerParams(
            dimension_semantics=("arbitrary",), vmem_limit_bytes=60 * 1024 * 1024
        ),
        name="attend",
    )(comp_lengths, prefix_len, q_lat, q_rope, grad_out, keys)


def reduce_kernel(ns, nd, nh, x_ref, o_ref, r1, y, r2, z, r3, u, sends, recvs):
    me_s = lax.axis_index("seq")
    me_d = lax.axis_index("dp")
    me_h = lax.axis_index("head")
    barrier = pltpu.get_barrier_semaphore()
    for axis, me, n in (("seq", me_s, ns), ("dp", me_d, nd), ("head", me_h, nh)):
        for off in range(1, n):
            pl.semaphore_signal(
                barrier, inc=1, device_id={axis: lax.rem(me + off, n)}, device_id_type=MESH
            )
    pl.semaphore_wait(barrier, ns + nd + nh - 3)

    count = [0]

    def exchange(axis, me, n, source, target):
        copies = []
        for off in range(1, n):
            peer = lax.rem(me + off, n)
            k = count[0]
            count[0] += 1
            copy = pltpu.make_async_remote_copy(
                src_ref=source(peer), dst_ref=target(off), send_sem=sends.at[k],
                recv_sem=recvs.at[k], device_id={axis: peer}, device_id_type=MESH,
            )
            copy.start()
            copies.append(copy)
        return copies

    pending = []
    copies = exchange("seq", me_s, ns, lambda p: x_ref.at[p], lambda off: r1.at[off - 1])
    total = x_ref[me_s].astype(F32)
    for off, copy in enumerate(copies):
        copy.wait_recv()
        total += r1[off].astype(F32)
    y[...] = total.astype(BF16)
    pending += copies

    copies = exchange("dp", me_d, nd, lambda p: y.at[:, p], lambda off: r2.at[off - 1])
    total = y[:, me_d].astype(F32)
    for off, copy in enumerate(copies):
        copy.wait_recv()
        total += r2[off].astype(F32)
    z[...] = total.astype(BF16)
    pending += copies

    copies = exchange("head", me_h, nh, lambda p: z.at[p], lambda off: r3.at[off - 1])
    total = z[me_h].astype(F32)
    for off, copy in enumerate(copies):
        copy.wait_recv()
        total += r3[off].astype(F32)
    u[...] = total.astype(BF16)
    pending += copies

    copies = exchange("dp", me_d, nd, lambda p: u, lambda off: o_ref.at[me_d])
    o_ref[me_d] = u[...]
    for copy in copies:
        copy.wait_recv()
    pending += copies
    for copy in pending:
        copy.wait_send()


def reduce_terms(terms):
    ns, nd, nh = (lax.axis_size(a) for a in ("seq", "dp", "head"))
    width = terms.shape[1]
    part = terms.shape[0] // (ns * nh * nd)
    x = terms.reshape(ns, nh, nd, part, width)
    total = ns + 2 * nd + nh - 4
    vmem = pl.BlockSpec(memory_space=pltpu.VMEM)
    out = pl.pallas_call(
        functools.partial(reduce_kernel, ns, nd, nh),
        out_shape=jax.ShapeDtypeStruct((nd, part, width), BF16),
        in_specs=[vmem],
        out_specs=vmem,
        scratch_shapes=[
            pltpu.VMEM((ns - 1, nh, nd, part, width), BF16),
            pltpu.VMEM((nh, nd, part, width), BF16),
            pltpu.VMEM((nd - 1, nh, part, width), BF16),
            pltpu.VMEM((nh, part, width), BF16),
            pltpu.VMEM((nh - 1, part, width), BF16),
            pltpu.VMEM((part, width), BF16),
            pltpu.SemaphoreType.DMA((total,)),
            pltpu.SemaphoreType.DMA((total,)),
        ],
        compiler_params=pltpu.CompilerParams(collective_id=0, has_side_effects=True),
        name="reduce_keys",
    )(x)
    return out.reshape(nd * part, width).T.astype(F32)


def on_device(q_lat, q_rope, grad_out, prefix_keys, comp_lengths, prefix_len):
    keys = lax.all_gather(prefix_keys, "seq", axis=1, tiled=True)
    dq_lat, dq_rope, terms = compute(q_lat, q_rope, grad_out, keys, comp_lengths, prefix_len)
    return dq_lat, dq_rope, reduce_terms(terms)


def solution(mesh):
    in_specs = (
        P(("dp", "seq"), "head"),
        P(("dp", "seq"), "head"),
        P(("dp", "seq"), "head"),
        P(None, "seq"),
        P(),
        P(),
    )
    out_specs = (P(("dp", "seq"), "head"), P(("dp", "seq"), "head"), P(None, ("seq", "head")))
    return jax.shard_map(
        on_device, mesh=mesh, in_specs=in_specs, out_specs=out_specs, check_vma=False
    )
```

time: 120 us -> 40.4 us (0.34)
  waiting for transfers between devices: 69.9 us -> 0 us
  Pallas kernels: 0 us -> 33.1 us
  local copies, waits for them, and re-layouts: 19.6 us -> 0 us
  between operations: 14.5 us -> 1.29 us
  matrix products: 9.83 us -> 0 us
  blocking collectives: 2.56 us -> 4.23 us
    psum x1 -> x0, waiting for transfers between devices: 40.8 us -> none  [on_device(): d_keys = lax.psum(portion, 'dp')]
    pallas_call x0 -> x2, Pallas kernels: none -> 33.1 us  [the longest x1 21.7 us: reduce_terms(): pl.pallas_call(functools.partial(reduce_kernel, ns, nd, nh), out_shape=ja...]
    unnamed x4 -> x0, waiting for transfers between devices: 17.9 us -> none
    reduce_scatter x1 -> x0, waiting for transfers between devices: 11.2 us -> none  [on_device(): by_seq = lax.psum_scatter(key_grads, 'seq', scatter_dimension=1, tiled=True)]
    reshape x5 -> x0, local copies, waits for them, and re-layouts: 11 us -> none  [the longest x1 3.73 us: on_device(): grad_out.reshape(rows, DL)]
    dot_general x8 -> x0, matrix products: 9.83 us -> none  [the longest x1 2.13 us: backward_step(): lax.dot_general(dscore_b, key_lat, contract_last, preferred_element_type=...]
    unnamed x9 -> x0, local copies, waits for them, and re-layouts: 6.33 us -> none
    convert_element_type x2 -> x0, local copies, waits for them, and re-layouts: 1.93 us -> none  [the longest x1 1.71 us: on_device(): (scale * grad_lat).astype(jnp.bfloat16).reshape(tok_rows, heads_here * DL)]
  transfers between devices with their start and end apart: 3 -> 0, of which waited for: 3 -> 0; matrix products, arithmetic and copies ran while one was open for 7% -> 0% of each run, Pallas kernels for 0% -> 0%
where the time goes in v1:
time: 40.4 us; the launch traced here: 40.1 us
  Pallas kernels  33.1 us (82%)
  blocking collectives  4.23 us (10%)
  other arithmetic  1.57 us (4%)
  between operations  1.29 us (3%)
    pallas_call x1, Pallas kernels, reduce_terms(): pl.pallas_call(functools.partial(reduce_kernel, ns, nd, nh), out_shape=ja...  21.7 us
    pallas_call x1, Pallas kernels, compute(): pl.pallas_call(functools.partial(compute_kernel, tok_rows), grid=(heads,)...  11.4 us
    all_gather x1, blocking collectives, on_device(): keys = lax.all_gather(prefix_keys, 'seq', axis=1, tiled=True)  4.23 us
    convert_element_type x1, other arithmetic, reduce_terms(): return out.reshape(nd * part, width).T.astype(F32)  1.57 us

profile of v1, /device:TPU:0, one launch (start us, length us, event | category | flops | bytes accessed | tf_op | source)
XLA Modules:
  0.0 40.1 jit_solution(6362079235183095222)
XLA Ops:
  1.3 4.2 %all_gather.3.keys_ref = bf16[576,512]{1,0:T(8,128)(2,1)} all-gather(bf16[576,256]{1,0:T(8,128)(2,1)} %param.9), channel_id=1, replica_groups=mesh['dp'=4,'seq'=2,'head'=4] {'seq'}, dimensions={1}, use_global_device_ids=true | all-gather | bytes 884736 | tf_op jit(solution)/shard_map/all_gather | solution.py:205
  5.5 11.4 %attend.1 = (bf16[384,2048]{1,0:T(8,128)(2,1)}, bf16[384,256]{1,0:T(8,128)(2,1)}, bf16[512,576]{1,0:T(8,128)(2,1)}) custom-call(s32[3]{0:T(128)} %lens_ref.1, s32[1]{0:T(128)S(6)} %copy.9.plen_ref, bf16[384,2048]{1,0:T(8,128)(2,1)} %q_ref.1, bf16[384,256]{1,0:T(8,128)(2,1)} %qr_ref.1, bf16[384,2048]{1,0:T(8,128)(2,1)} %g_ref.1, ...), custom_call_target="tpu_custom_call" | custom-call | tf_op jit(solution)/shard_map/attend/pallas_call | solution.py:90
  16.9 21.7 %reduce_keys.1 = bf16[4,16,576]{2,1,0:T(8,128)(2,1)} custom-call(bf16[2,4,4,16,576]{4,3,2,1,0:T(8,128)(2,1)} %bitcast.6), custom_call_target="tpu_custom_call" | custom-call | tf_op jit(solution)/shard_map/reduce_keys/pallas_call | solution.py:183
  38.6 1.6 %convert_bitcast_fusion = f32[576,64]{0,1:T(8,128)} fusion(bf16[4,16,576]{2,1,0:T(8,128)(2,1)} %reduce_keys.1), kind=kLoop, calls=%fused_computation | loop fusion | flops 36864 | bytes 221184 | tf_op jit(solution)/shard_map/convert_element_type | solution.py:201

commit v2 on v1

--- a/solution.py
+++ b/solution.py
@@ -20,20 +20,54 @@
     return lax.dot_general(a, b, (((da,), (db,)), ((), ())), preferred_element_type=F32)
 
 
+def head_step(used, parity, scale, g, plen_ref, q_ref, qr_ref,
+              dq_ref, dqr_ref, keys_t, rope_t, acc_p, acc_q, acc_r):
+    q = q_ref[...]
+    qr = qr_ref[...]
+    kt = keys_t[:used]
+    rt = rope_t[parity, :used]
+    s = (dot(kt, q, 1, 1) + dot(rt, qr, 1, 1)) * scale
+    keep = lax.broadcasted_iota(jnp.int32, (used, 1), 0) < plen_ref[0]
+    s = jnp.where(keep, s, NEG)
+    e = jnp.exp(s - jnp.max(s, axis=0, keepdims=True))
+    inv = 1.0 / jnp.sum(e, axis=0, keepdims=True)
+    dp = dot(kt, g, 1, 1)
+    p = e * inv
+    delta = jnp.sum(p * dp, axis=0, keepdims=True)
+    ds = (p * (dp - delta)).astype(BF16)
+    acc_p[:used] += dot(p.astype(BF16), g, 1, 0)
+    acc_q[:used] += dot(ds, q, 1, 0)
+    acc_r[parity, :used] += dot(ds, qr, 1, 0)
+    dst = ds.T
+    dq_ref[...] = (scale * dot(dst, kt, 1, 0)).astype(BF16)
+    half = (scale * dot(dst, rt, 1, 0)).astype(BF16)
+
+    @pl.when(parity == 0)
+    def _():
+        dqr_ref[...] = half
+
+    @pl.when(parity == 1)
+    def _():
+        dqr_ref[...] += half
+
+
 def compute_kernel(tok_rows, lens_ref, plen_ref, q_ref, qr_ref, g_ref, keys_ref,
                    dq_ref, dqr_ref, terms_ref, keys_t, rope_t, acc_p, acc_q, acc_r):
     head = pl.program_id(0)
     parity = lax.rem(head, 2)
     scale = (DL + DR) ** (-0.5)
-    cols = keys_ref.shape[1]
+    parts, _, wide = keys_ref.shape
+    cols = parts * wide
 
     @pl.when(head == 0)
     def _():
-        keys_t[...] = keys_ref[:DL].T
-        rope = keys_ref[DL:].astype(F32).T
-        zero = jnp.zeros_like(rope)
-        rope_t[0] = jnp.concatenate([rope, zero], axis=1).astype(BF16)
-        rope_t[1] = jnp.concatenate([zero, rope], axis=1).astype(BF16)
+        for part in range(parts):
+            rows = pl.ds(part * wide, wide)
+            keys_t[rows] = keys_ref[part, :DL].T
+            rope = keys_ref[part, DL:].astype(F32).T
+            zero = jnp.zeros_like(rope)
+            rope_t[0, rows] = jnp.concatenate([rope, zero], axis=1).astype(BF16)
+            rope_t[1, rows] = jnp.concatenate([zero, rope], axis=1).astype(BF16)
         acc_p[...] = jnp.zeros_like(acc_p)
         acc_q[...] = jnp.zeros_like(acc_q)
         acc_r[...] = jnp.zeros_like(acc_r)
@@ -46,33 +80,15 @@
         length = jnp.where(comp == c, lens_ref[c], length)
     valid = tok - comp * CLEN < length
     g = jnp.where(valid, g_ref[...].astype(F32), 0.0).astype(BF16)
-    q = q_ref[...]
-    qr = qr_ref[...]
-    kt = keys_t[...]
-    rt = rope_t[parity]
-    s = (dot(kt, q, 1, 1) + dot(rt, qr, 1, 1)) * scale
-    keep = lax.broadcasted_iota(jnp.int32, (cols, 1), 0) < plen_ref[0]
-    s = jnp.where(keep, s, NEG)
-    e = jnp.exp(s - jnp.max(s, axis=0, keepdims=True))
-    inv = 1.0 / jnp.sum(e, axis=0, keepdims=True)
-    dp = dot(kt, g, 1, 1)
-    p = e * inv
-    delta = jnp.sum(p * dp, axis=0, keepdims=True)
-    ds = (p * (dp - delta)).astype(BF16)
-    acc_p[...] += dot(p.astype(BF16), g, 1, 0)
-    acc_q[...] += dot(ds, q, 1, 0)
-    acc_r[parity] += dot(ds, qr, 1, 0)
-    dst = ds.T
-    dq_ref[...] = (scale * dot(dst, kt, 1, 0)).astype(BF16)
-    half = (scale * dot(dst, rt, 1, 0)).astype(BF16)
-
-    @pl.when(parity == 0)
-    def _():
-        dqr_ref[...] = half
-
-    @pl.when(parity == 1)
-    def _():
-        dqr_ref[...] += half
+    step = cols // 4 if cols % 512 == 0 else cols
+    blocks = (plen_ref[0] + step - 1) // step
+
+    for used in range(step, cols + 1, step):
+
+        @pl.when(blocks == used // step)
+        def _():
+            head_step(used, parity, scale, g, plen_ref, q_ref, qr_ref,
+                      dq_ref, dqr_ref, keys_t, rope_t, acc_p, acc_q, acc_r)
 
     @pl.when(head == pl.num_programs(0) - 1)
     def _():
@@ -83,7 +99,7 @@
 def compute(q_lat, q_rope, grad_out, keys, comp_lengths, prefix_len):
     tok_rows = q_lat.shape[0]
     heads = q_lat.shape[1] // DL
-    cols = keys.shape[1]
+    cols = keys.shape[0] * keys.shape[2]
     lat = pl.BlockSpec((tok_rows, DL), lambda h: (0, h))
     rope = pl.BlockSpec((tok_rows, 2 * DR), lambda h: (0, h // 2))
     smem = pl.BlockSpec(memory_space=pltpu.SMEM)
@@ -95,7 +111,7 @@
             jax.ShapeDtypeStruct(q_rope.shape, BF16),
             jax.ShapeDtypeStruct((cols, DL + DR), BF16),
         ),
-        in_specs=[smem, smem, lat, rope, lat, pl.BlockSpec((DL + DR, cols), lambda h: (0, 0))],
+        in_specs=[smem, smem, lat, rope, lat, pl.BlockSpec(keys.shape, lambda h: (0, 0, 0))],
         out_specs=(lat, rope, pl.BlockSpec((cols, DL + DR), lambda h: (0, 0))),
         scratch_shapes=[
             pltpu.VMEM((cols, DL), BF16),
@@ -171,6 +187,45 @@
     pending += copies
     for copy in pending:
         copy.wait_send()
+
+
+def widen_kernel(x_ref, o_ref):
+    o_ref[...] = x_ref[...].astype(F32)
+
+
+def gather_kernel(ns, x_ref, o_ref, sends, recvs):
+    me = lax.axis_index("seq")
+    barrier = pltpu.get_barrier_semaphore()
+    peers = [lax.rem(me + off, ns) for off in range(1, ns)]
+    for peer in peers:
+        pl.semaphore_signal(barrier, inc=1, device_id={"seq": peer}, device_id_type=MESH)
+    pl.semaphore_wait(barrier, ns - 1)
+    copies = [
+        pltpu.make_async_remote_copy(
+            src_ref=x_ref, dst_ref=o_ref.at[me], send_sem=sends.at[k], recv_sem=recvs.at[k],
+            device_id={"seq": peer}, device_id_type=MESH,
+        )
+        for k, peer in enumerate(peers)
+    ]
+    for copy in copies:
+        copy.start()
+    o_ref[me] = x_ref[...]
+    for copy in copies:
+        copy.wait()
+
+
+def gather(keys):
+    ns = lax.axis_size("seq")
+    vmem = pl.BlockSpec(memory_space=pltpu.VMEM)
+    return pl.pallas_call(
+        functools.partial(gather_kernel, ns),
+        out_shape=jax.ShapeDtypeStruct((ns, *keys.shape), keys.dtype),
+        in_specs=[vmem],
+        out_specs=vmem,
+        scratch_shapes=[pltpu.SemaphoreType.DMA((ns - 1,)), pltpu.SemaphoreType.DMA((ns - 1,))],
+        compiler_params=pltpu.CompilerParams(collective_id=1, has_side_effects=True),
+        name="gather_keys",
+    )(keys)
 
 
 def reduce_terms(terms):
@@ -198,11 +253,17 @@
         compiler_params=pltpu.CompilerParams(collective_id=0, has_side_effects=True),
         name="reduce_keys",
     )(x)
-    return out.reshape(nd * part, width).T.astype(F32)
+    return pl.pallas_call(
+        widen_kernel,
+        out_shape=jax.ShapeDtypeStruct((nd * part, width), F32),
+        in_specs=[vmem],
+        out_specs=vmem,
+        name="widen",
+    )(out.reshape(nd * part, width)).T
 
 
 def on_device(q_lat, q_rope, grad_out, prefix_keys, comp_lengths, prefix_len):
-    keys = lax.all_gather(prefix_keys, "seq", axis=1, tiled=True)
+    keys = gather(prefix_keys)
     dq_lat, dq_rope, terms = compute(q_lat, q_rope, grad_out, keys, comp_lengths, prefix_len)
     return dq_lat, dq_rope, reduce_terms(terms)
 

time: 40.4 us -> 37.4 us (0.926)
  blocking collectives: 4.23 us -> 0 us
  Pallas kernels: 33.1 us -> 35.9 us
  other arithmetic: 1.57 us -> 0 us
    pallas_call x0 -> x2, Pallas kernels: none -> 5.1 us  [the longest x1 3.54 us: gather(): pl.pallas_call(functools.partial(gather_kernel, ns), out_shape=jax.ShapeD...]
    all_gather x1 -> x0, blocking collectives: 4.23 us -> none  [on_device(): keys = lax.all_gather(prefix_keys, 'seq', axis=1, tiled=True)]
    pallas_call x1, Pallas kernels: 11.4 us -> 8.87 us  [compute(): pl.pallas_call(functools.partial(compute_kernel, tok_rows), grid=(heads,)...]
    convert_element_type x1 -> x0, other arithmetic: 1.57 us -> none  [reduce_terms(): return out.reshape(nd * part, width).T.astype(F32)]
where the time goes in v2:
time: 37.4 us; the launch traced here: 37.2 us
  Pallas kernels  35.9 us (96%)
  between operations  1.3 us (3%)
    pallas_call x1, Pallas kernels, reduce_terms(): pl.pallas_call(functools.partial(reduce_kernel, ns, nd, nh), out_shape=ja...  21.9 us
    pallas_call x1, Pallas kernels, compute(): pl.pallas_call(functools.partial(compute_kernel, tok_rows), grid=(heads,)...  8.87 us
    pallas_call x1, Pallas kernels, gather(): pl.pallas_call(functools.partial(gather_kernel, ns), out_shape=jax.ShapeD...  3.54 us
    pallas_call x1, Pallas kernels, reduce_terms(): pl.pallas_call(widen_kernel, out_shape=jax.ShapeDtypeStruct((nd * part, w...  1.57 us

profile of v2, /device:TPU:0, one launch (start us, length us, event | category | flops | bytes accessed | tf_op | source)
XLA Modules:
  0.0 37.2 jit_solution(11931895030126472174)
XLA Ops:
  1.3 3.5 %gather_keys.1.keys_ref = bf16[2,576,256]{2,1,0:T(8,128)(2,1)} custom-call(bf16[576,256]{1,0:T(8,128)(2,1)} %x_ref.1), custom_call_target="tpu_custom_call" | custom-call | tf_op jit(solution)/shard_map/gather_keys/pallas_call | solution.py:220
  4.8 8.9 %attend.1 = (bf16[384,2048]{1,0:T(8,128)(2,1)}, bf16[384,256]{1,0:T(8,128)(2,1)}, bf16[512,576]{1,0:T(8,128)(2,1)}) custom-call(s32[3]{0:T(128)} %lens_ref.1, s32[1]{0:T(128)S(6)} %copy.9.plen_ref, bf16[384,2048]{1,0:T(8,128)(2,1)} %q_ref.1, bf16[384,256]{1,0:T(8,128)(2,1)} %qr_ref.1, bf16[384,2048]{1,0:T(8,128)(2,1)} %g_ref.1, ...), custom_call_target="tpu_custom_call" | custom-call | tf_op jit(solution)/shard_map/attend/pallas_call | solution.py:106
  13.7 21.9 %reduce_keys.1 = bf16[4,16,576]{2,1,0:T(8,128)(2,1)} custom-call(bf16[2,4,4,16,576]{4,3,2,1,0:T(8,128)(2,1)} %bitcast.3), custom_call_target="tpu_custom_call" | custom-call | tf_op jit(solution)/shard_map/reduce_keys/pallas_call | solution.py:238
  35.6 1.6 %widen.1 = f32[64,576]{1,0:T(8,128)} custom-call(bf16[64,576]{1,0:T(8,128)(2,1)} %bitcast.4), custom_call_target="tpu_custom_call" | custom-call | tf_op jit(solution)/shard_map/widen/pallas_call | solution.py:256

commit v3 on v2

--- a/solution.py
+++ b/solution.py
@@ -20,12 +20,10 @@
     return lax.dot_general(a, b, (((da,), (db,)), ((), ())), preferred_element_type=F32)
 
 
-def head_step(used, parity, scale, g, plen_ref, q_ref, qr_ref,
-              dq_ref, dqr_ref, keys_t, rope_t, acc_p, acc_q, acc_r):
-    q = q_ref[...]
-    qr = qr_ref[...]
+def pair_step(used, scale, g, q, qr, plen_ref, dq_ref, dqr_ref, keys_t, rope_t, acc_p, acc_q, acc_r):
+    tok_rows = dq_ref.shape[0]
     kt = keys_t[:used]
-    rt = rope_t[parity, :used]
+    rt = rope_t[:used]
     s = (dot(kt, q, 1, 1) + dot(rt, qr, 1, 1)) * scale
     keep = lax.broadcasted_iota(jnp.int32, (used, 1), 0) < plen_ref[0]
     s = jnp.where(keep, s, NEG)
@@ -37,24 +35,19 @@
     ds = (p * (dp - delta)).astype(BF16)
     acc_p[:used] += dot(p.astype(BF16), g, 1, 0)
     acc_q[:used] += dot(ds, q, 1, 0)
-    acc_r[parity, :used] += dot(ds, qr, 1, 0)
+    acc_r[:used] += dot(ds, qr, 1, 0)
     dst = ds.T
-    dq_ref[...] = (scale * dot(dst, kt, 1, 0)).astype(BF16)
-    half = (scale * dot(dst, rt, 1, 0)).astype(BF16)
-
-    @pl.when(parity == 0)
-    def _():
-        dqr_ref[...] = half
-
-    @pl.when(parity == 1)
-    def _():
-        dqr_ref[...] += half
+    dq = (scale * dot(dst, kt, 1, 0)).astype(BF16)
+    dq_ref[:, :DL] = dq[:tok_rows]
+    dq_ref[:, DL:] = dq[tok_rows:]
+    both = scale * dot(dst, rt, 1, 0)
+    left = lax.broadcasted_iota(jnp.int32, (1, 2 * DR), 1) < DR
+    dqr_ref[...] = jnp.where(left, both[:tok_rows], both[tok_rows:]).astype(BF16)
 
 
 def compute_kernel(tok_rows, lens_ref, plen_ref, q_ref, qr_ref, g_ref, keys_ref,
                    dq_ref, dqr_ref, terms_ref, keys_t, rope_t, acc_p, acc_q, acc_r):
     head = pl.program_id(0)
-    parity = lax.rem(head, 2)
     scale = (DL + DR) ** (-0.5)
     parts, _, wide = keys_ref.shape
     cols = parts * wide
@@ -65,9 +58,7 @@
             rows = pl.ds(part * wide, wide)
             keys_t[rows] = keys_ref[part, :DL].T
             rope = keys_ref[part, DL:].astype(F32).T
-            zero = jnp.zeros_like(rope)
-            rope_t[0, rows] = jnp.concatenate([rope, zero], axis=1).astype(BF16)
-            rope_t[1, rows] = jnp.concatenate([zero, rope], axis=1).astype(BF16)
+            rope_t[rows] = jnp.concatenate([rope, rope], axis=1).astype(BF16)
         acc_p[...] = jnp.zeros_like(acc_p)
         acc_q[...] = jnp.zeros_like(acc_q)
         acc_r[...] = jnp.zeros_like(acc_r)
@@ -80,6 +71,11 @@
         length = jnp.where(comp == c, lens_ref[c], length)
     valid = tok - comp * CLEN < length
     g = jnp.where(valid, g_ref[...].astype(F32), 0.0).astype(BF16)
+    g = jnp.concatenate([g[:, :DL], g[:, DL:]], axis=0)
+    q = jnp.concatenate([q_ref[:, :DL], q_ref[:, DL:]], axis=0)
+    qr = qr_ref[...].astype(F32)
+    left = lax.broadcasted_iota(jnp.int32, (1, 2 * DR), 1) < DR
+    qr = jnp.concatenate([jnp.where(left, qr, 0.0), jnp.where(left, 0.0, qr)], axis=0).astype(BF16)
     step = cols // 4 if cols % 512 == 0 else cols
     blocks = (plen_ref[0] + step - 1) // step
 
@@ -87,25 +83,25 @@
 
         @pl.when(blocks == used // step)
         def _():
-            head_step(used, parity, scale, g, plen_ref, q_ref, qr_ref,
-                      dq_ref, dqr_ref, keys_t, rope_t, acc_p, acc_q, acc_r)
+            pair_step(used, scale, g, q, qr, plen_ref, dq_ref, dqr_ref,
+                      keys_t, rope_t, acc_p, acc_q, acc_r)
 
     @pl.when(head == pl.num_programs(0) - 1)
     def _():
         terms_ref[:, :DL] = (acc_p[...] + scale * acc_q[...]).astype(BF16)
-        terms_ref[:, DL:] = (scale * (acc_r[0][:, :DR] + acc_r[1][:, DR:])).astype(BF16)
+        terms_ref[:, DL:] = (scale * (acc_r[:, :DR] + acc_r[:, DR:])).astype(BF16)
 
 
 def compute(q_lat, q_rope, grad_out, keys, comp_lengths, prefix_len):
     tok_rows = q_lat.shape[0]
     heads = q_lat.shape[1] // DL
     cols = keys.shape[0] * keys.shape[2]
-    lat = pl.BlockSpec((tok_rows, DL), lambda h: (0, h))
-    rope = pl.BlockSpec((tok_rows, 2 * DR), lambda h: (0, h // 2))
+    lat = pl.BlockSpec((tok_rows, 2 * DL), lambda h: (0, h))
+    rope = pl.BlockSpec((tok_rows, 2 * DR), lambda h: (0, h))
     smem = pl.BlockSpec(memory_space=pltpu.SMEM)
     return pl.pallas_call(
         functools.partial(compute_kernel, tok_rows),
-        grid=(heads,),
+        grid=(heads // 2,),
         out_shape=(
             jax.ShapeDtypeStruct(q_lat.shape, BF16),
             jax.ShapeDtypeStruct(q_rope.shape, BF16),
@@ -115,10 +111,10 @@
         out_specs=(lat, rope, pl.BlockSpec((cols, DL + DR), lambda h: (0, 0))),
         scratch_shapes=[
             pltpu.VMEM((cols, DL), BF16),
-            pltpu.VMEM((2, cols, 2 * DR), BF16),
+            pltpu.VMEM((cols, 2 * DR), BF16),
             pltpu.VMEM((cols, DL), F32),
             pltpu.VMEM((cols, DL), F32),
-            pltpu.VMEM((2, cols, 2 * DR), F32),
+            pltpu.VMEM((cols, 2 * DR), F32),
         ],
         compiler_params=pltpu.CompilerParams(
             dimension_semantics=("arbitrary",), vmem_limit_bytes=60 * 1024 * 1024
@@ -127,19 +123,23 @@
     )(comp_lengths, prefix_len, q_lat, q_rope, grad_out, keys)
 
 
-def reduce_kernel(ns, nd, nh, x_ref, o_ref, r1, y, r2, z, r3, u, sends, recvs):
+def reduce_kernel(ns, nd, nh, cuts, src_ref, o_ref, x_ref, r1, y, r2, z, r3, u, sends, recvs, load):
     me_s = lax.axis_index("seq")
     me_d = lax.axis_index("dp")
     me_h = lax.axis_index("head")
+    copy_in = pltpu.make_async_copy(src_ref, x_ref, load)
+    copy_in.start()
     barrier = pltpu.get_barrier_semaphore()
     for axis, me, n in (("seq", me_s, ns), ("dp", me_d, nd), ("head", me_h, nh)):
         for off in range(1, n):
             pl.semaphore_signal(
                 barrier, inc=1, device_id={axis: lax.rem(me + off, n)}, device_id_type=MESH
             )
+    copy_in.wait()
     pl.semaphore_wait(barrier, ns + nd + nh - 3)
 
     count = [0]
+    pending = []
 
     def exchange(axis, me, n, source, target):
         copies = []
@@ -153,38 +153,40 @@
             )
             copy.start()
             copies.append(copy)
+        pending.extend(copies)
         return copies
 
-    pending = []
-    copies = exchange("seq", me_s, ns, lambda p: x_ref.at[p], lambda off: r1.at[off - 1])
-    total = x_ref[me_s].astype(F32)
-    for off, copy in enumerate(copies):
-        copy.wait_recv()
-        total += r1[off].astype(F32)
-    y[...] = total.astype(BF16)
-    pending += copies
-
-    copies = exchange("dp", me_d, nd, lambda p: y.at[:, p], lambda off: r2.at[off - 1])
-    total = y[:, me_d].astype(F32)
-    for off, copy in enumerate(copies):
-        copy.wait_recv()
-        total += r2[off].astype(F32)
-    z[...] = total.astype(BF16)
-    pending += copies
-
-    copies = exchange("head", me_h, nh, lambda p: z.at[p], lambda off: r3.at[off - 1])
-    total = z[me_h].astype(F32)
-    for off, copy in enumerate(copies):
-        copy.wait_recv()
-        total += r3[off].astype(F32)
-    u[...] = total.astype(BF16)
-    pending += copies
-
-    copies = exchange("dp", me_d, nd, lambda p: u, lambda off: o_ref.at[me_d])
+    def summed(own, landed, copies):
+        total = own.astype(F32)
+        for off, copy in enumerate(copies):
+            copy.wait_recv()
+            total += landed(off).astype(F32)
+        return total.astype(BF16)
+
+    lanes = [pl.ds(lo, hi - lo) for lo, hi in cuts]
+    stage = [
+        exchange("seq", me_s, ns, lambda p, c=c: x_ref.at[p, :, :, :, c],
+                 lambda off, c=c: r1.at[off - 1, :, :, :, c])
+        for c in lanes
+    ]
+    after = []
+    for c, copies in zip(lanes, stage):
+        y[:, :, :, c] = summed(x_ref[me_s, :, :, :, c], lambda off: r1[off, :, :, :, c], copies)
+        after.append(exchange("dp", me_d, nd, lambda p: y.at[:, p, :, c],
+                              lambda off: r2.at[off - 1, :, :, c]))
+    stage, after = after, []
+    for c, copies in zip(lanes, stage):
+        z[:, :, c] = summed(y[:, me_d, :, c], lambda off: r2[off, :, :, c], copies)
+        after.append(exchange("head", me_h, nh, lambda p: z.at[p, :, c],
+                              lambda off: r3.at[off - 1, :, c]))
+    stage, after = after, []
+    for c, copies in zip(lanes, stage):
+        u[:, c] = summed(z[me_h, :, c], lambda off: r3[off, :, c], copies)
+        after.append(exchange("dp", me_d, nd, lambda p: u.at[:, c], lambda off: o_ref.at[me_d, :, c]))
     o_ref[me_d] = u[...]
-    for copy in copies:
-        copy.wait_recv()
-    pending += copies
+    for copies in after:
+        for copy in copies:
+            copy.wait_recv()
     for copy in pending:
         copy.wait_send()
 
@@ -233,14 +235,16 @@
     width = terms.shape[1]
     part = terms.shape[0] // (ns * nh * nd)
     x = terms.reshape(ns, nh, nd, part, width)
-    total = ns + 2 * nd + nh - 4
+    cuts = ((0, DL // 2), (DL // 2, width))
+    total = (ns + 2 * nd + nh - 4) * len(cuts)
     vmem = pl.BlockSpec(memory_space=pltpu.VMEM)
     out = pl.pallas_call(
-        functools.partial(reduce_kernel, ns, nd, nh),
+        functools.partial(reduce_kernel, ns, nd, nh, cuts),
         out_shape=jax.ShapeDtypeStruct((nd, part, width), BF16),
-        in_specs=[vmem],
+        in_specs=[pl.BlockSpec(memory_space=pl.ANY)],
         out_specs=vmem,
         scratch_shapes=[
+            pltpu.VMEM((ns, nh, nd, part, width), BF16),
             pltpu.VMEM((ns - 1, nh, nd, part, width), BF16),
             pltpu.VMEM((nh, nd, part, width), BF16),
             pltpu.VMEM((nd - 1, nh, part, width), BF16),
@@ -249,6 +253,7 @@
             pltpu.VMEM((part, width), BF16),
             pltpu.SemaphoreType.DMA((total,)),
             pltpu.SemaphoreType.DMA((total,)),
+            pltpu.SemaphoreType.DMA,
         ],
         compiler_params=pltpu.CompilerParams(collective_id=0, has_side_effects=True),
         name="reduce_keys",

time: 37.4 us -> 34.7 us (0.928)
  Pallas kernels: 35.9 us -> 33.1 us
    pallas_call x2, Pallas kernels: 30.8 us -> 28 us  [the longest x1 20.5 us: reduce_terms(): pl.pallas_call(functools.partial(reduce_kernel, ns, nd, nh, cuts), out_sh...]
where the time goes in v3:
time: 34.7 us; the launch traced here: 34.4 us
  Pallas kernels  33.1 us (95%)
  between operations  1.3 us (4%)
    pallas_call x1, Pallas kernels, reduce_terms(): pl.pallas_call(functools.partial(reduce_kernel, ns, nd, nh, cuts), out_sh...  20.5 us
    pallas_call x1, Pallas kernels, compute(): pl.pallas_call(functools.partial(compute_kernel, tok_rows), grid=(heads /...  7.54 us
    pallas_call x1, Pallas kernels, gather(): pl.pallas_call(functools.partial(gather_kernel, ns), out_shape=jax.ShapeD...  3.54 us
    pallas_call x1, Pallas kernels, reduce_terms(): pl.pallas_call(widen_kernel, out_shape=jax.ShapeDtypeStruct((nd * part, w...  1.57 us

profile of v3, /device:TPU:0, one launch (start us, length us, event | category | flops | bytes accessed | tf_op | source)
XLA Modules:
  0.0 34.4 jit_solution(775667426369485427)
XLA Ops:
  1.3 3.5 %gather_keys.1.keys_ref = bf16[2,576,256]{2,1,0:T(8,128)(2,1)} custom-call(bf16[576,256]{1,0:T(8,128)(2,1)} %x_ref.1), custom_call_target="tpu_custom_call" | custom-call | tf_op jit(solution)/shard_map/gather_keys/pallas_call | solution.py:222
  4.8 7.5 %attend.1 = (bf16[384,2048]{1,0:T(8,128)(2,1)}, bf16[384,256]{1,0:T(8,128)(2,1)}, bf16[512,576]{1,0:T(8,128)(2,1)}) custom-call(s32[3]{0:T(128)} %lens_ref.1, s32[1]{0:T(128)S(6)} %copy.9.plen_ref, bf16[384,2048]{1,0:T(8,128)(2,1)} %q_ref.1, bf16[384,256]{1,0:T(8,128)(2,1)} %qr_ref.1, bf16[384,2048]{1,0:T(8,128)(2,1)} %g_ref.1, ...), custom_call_target="tpu_custom_call" | custom-call | tf_op jit(solution)/shard_map/attend/pallas_call | solution.py:102
  12.4 20.5 %reduce_keys.1 = bf16[4,16,576]{2,1,0:T(8,128)(2,1)} custom-call(bf16[2,4,4,16,576]{4,3,2,1,0:T(8,128)(2,1)} %bitcast.3), custom_call_target="tpu_custom_call" | custom-call | tf_op jit(solution)/shard_map/reduce_keys/pallas_call | solution.py:241
  32.9 1.6 %widen.1 = f32[64,576]{1,0:T(8,128)} custom-call(bf16[64,576]{1,0:T(8,128)(2,1)} %bitcast.4), custom_call_target="tpu_custom_call" | custom-call | tf_op jit(solution)/shard_map/widen/pallas_call | solution.py:261
